TPU v7x, 16 devices: a whole 2x2x2 slice. The times are simulated.
16 devices in a mesh: sp: 16 (over z, y, x, core).
Axes of the slice: x: 2, y: 2, z: 2, core: 2. Of those that a mesh axis runs over, the one named last changes fastest.
Arguments:
- x_in: bfloat16 [8, 1024, 4096], P(None, 'sp')
- dy_in: bfloat16 [8, 1024, 4096], P(None, 'sp')
- w_qkv: bfloat16 [4096, 8, 6, 128], replicated
- w_out: bfloat16 [4096, 4096], replicated
- ln_gain: float32 [4096], replicated
- ln_bias: float32 [4096], replicated
- positions: int32 [1024], P('sp')
Outputs:
- output 1: bfloat16 [8, 1024, 4096], P(None, 'sp')
- output 2: bfloat16 [8, 1024, 4096], P(None, 'sp')
- output 3: float32 [4096, 8, 6, 128], replicated
- output 4: float32 [4096, 4096], replicated
- output 5: float32 [4096], replicated
- output 6: float32 [4096], replicated
All inputs are finite; a program needn't handle non-finite values.
Results may differ from a plain program's by a relative error of at most 0.0153087.
Values are sent between devices in bfloat16 or wider.
A program may use at most 1.25 GiB of HBM per device.

v0:
```python
import jax
import jax.numpy as jnp
from jax import lax
from jax.sharding import PartitionSpec as P, NamedSharding

LN_EPS = 1e-5
ROPE_BASE = 10000.0


def layer_norm(x_rows, ln_gain, ln_bias):
    x_f32 = x_rows.astype(jnp.float32)
    centered = x_f32 - jnp.mean(x_f32, axis=-1, keepdims=True)
    variance = jnp.mean(centered * centered, axis=-1, keepdims=True)
    return (centered * lax.rsqrt(variance + LN_EPS) * ln_gain + ln_bias).astype(jnp.bfloat16)


def rope_tables(positions, head_dim):
    exponents = jnp.arange(head_dim // 2, dtype=jnp.float32) * (2.0 / head_dim)
    inv_freq = jnp.power(ROPE_BASE, -exponents)
    angles = positions.astype(jnp.float32)[:, None] * inv_freq[None, :]
    return jnp.cos(angles), jnp.sin(angles)


def rotate(t_in, cos_tab, sin_tab):
    half_dim = t_in.shape[-1] // 2
    t_f32 = t_in.astype(jnp.float32)
    first_half = t_f32[..., :half_dim]
    second_half = t_f32[..., half_dim:]
    cos_b = cos_tab[None, :, None, :]
    sin_b = sin_tab[None, :, None, :]
    return jnp.concatenate([first_half * cos_b - second_half * sin_b, second_half * cos_b + first_half * sin_b], axis=-1).astype(jnp.bfloat16)


def solution(mesh):
    sp_size = mesh.shape['sp']
    seq_spec = P(None, 'sp', None)

    def per_device(x_loc, dy_loc, w_qkv, w_out, ln_gain, ln_bias, pos_loc):
        batch_size, seq_loc = x_loc.shape[0], x_loc.shape[1]
        kv_heads = w_qkv.shape[1]
        group_q = w_qkv.shape[2] - 2
        head_dim = w_qkv.shape[3]
        num_heads = kv_heads * group_q
        kv_copies = max(1, sp_size // kv_heads)
        kv_local = max(1, kv_heads // sp_size)
        q_local = num_heads // sp_size
        q_per_kv = q_local // kv_local
        seq_all = seq_loc * sp_size
        score_scale = head_dim ** -0.5
        cos_tab, sin_tab = rope_tables(pos_loc, head_dim)
        causal = jnp.arange(seq_all)[:, None, None] >= jnp.arange(seq_all)[None, None, :]

        h_norm, ln_back = jax.vjp(layer_norm, x_loc, ln_gain, ln_bias)
        qkv_act = jnp.einsum('bsd,dgjh->bsgjh', h_norm, w_qkv, preferred_element_type=jnp.float32).astype(jnp.bfloat16)
        q_rot = rotate(qkv_act[:, :, :, :group_q, :].reshape(batch_size, seq_loc, num_heads, head_dim), cos_tab, sin_tab)
        k_send = jnp.repeat(rotate(qkv_act[:, :, :, group_q, :], cos_tab, sin_tab), kv_copies, axis=2)
        v_send = jnp.repeat(qkv_act[:, :, :, group_q + 1, :], kv_copies, axis=2)

        q_heads = lax.all_to_all(q_rot, 'sp', 2, 1, tiled=True).reshape(batch_size, seq_all, kv_local, q_per_kv, head_dim)
        k_heads = lax.all_to_all(k_send, 'sp', 2, 1, tiled=True)
        v_heads = lax.all_to_all(v_send, 'sp', 2, 1, tiled=True)

        scores = jnp.einsum('bqgjh,bkgh->bgqjk', q_heads, k_heads, preferred_element_type=jnp.float32) * score_scale
        attn_probs = jax.nn.softmax(jnp.where(causal, scores, -jnp.inf), axis=-1)
        probs_b = attn_probs.astype(jnp.bfloat16)
        head_ctx = jnp.einsum('bgqjk,bkgh->bqgjh', probs_b, v_heads, preferred_element_type=jnp.float32).astype(jnp.bfloat16)
        ctx_loc = lax.all_to_all(head_ctx.reshape(batch_size, seq_all, q_local, head_dim), 'sp', 1, 2, tiled=True)
        ctx_loc = ctx_loc.reshape(batch_size, seq_loc, num_heads * head_dim)
        attn_out = jnp.einsum('bsc,cd->bsd', ctx_loc, w_out, preferred_element_type=jnp.float32).astype(jnp.bfloat16)

        grad_w_out = jnp.einsum('bsc,bsd->cd', ctx_loc, dy_loc, preferred_element_type=jnp.float32)
        grad_ctx = jnp.einsum('bsd,cd->bsc', dy_loc, w_out, preferred_element_type=jnp.float32).astype(jnp.bfloat16)
        grad_heads = lax.all_to_all(grad_ctx.reshape(batch_size, seq_loc, num_heads, head_dim), 'sp', 2, 1, tiled=True)
        grad_heads = grad_heads.reshape(batch_size, seq_all, kv_local, q_per_kv, head_dim)
        grad_v_heads = jnp.einsum('bgqjk,bqgjh->bkgh', probs_b, grad_heads, preferred_element_type=jnp.float32).astype(jnp.bfloat16)
        grad_probs = jnp.einsum('bqgjh,bkgh->bgqjk', grad_heads, v_heads, preferred_element_type=jnp.float32).astype(jnp.bfloat16)
        row_dot = jnp.sum(grad_probs * attn_probs, axis=-1, keepdims=True)
        grad_scores = (attn_probs * (grad_probs - row_dot) * score_scale).astype(jnp.bfloat16)
        grad_q_heads = jnp.einsum('bgqjk,bkgh->bqgjh', grad_scores, k_heads, preferred_element_type=jnp.float32).astype(jnp.bfloat16)
        grad_k_heads = jnp.einsum('bgqjk,bqgjh->bkgh', grad_scores, q_heads, preferred_element_type=jnp.float32).astype(jnp.bfloat16)

        grad_q_rot = lax.all_to_all(grad_q_heads.reshape(batch_size, seq_all, q_local, head_dim), 'sp', 1, 2, tiled=True)
        grad_k_back = lax.all_to_all(grad_k_heads, 'sp', 1, 2, tiled=True)
        grad_v_back = lax.all_to_all(grad_v_heads, 'sp', 1, 2, tiled=True)
        grad_k_rot = jnp.sum(grad_k_back.reshape(batch_size, seq_loc, kv_heads, kv_copies, head_dim).astype(jnp.float32), axis=3).astype(jnp.bfloat16)
        grad_v = jnp.sum(grad_v_back.reshape(batch_size, seq_loc, kv_heads, kv_copies, head_dim).astype(jnp.float32), axis=3).astype(jnp.bfloat16)
        grad_q = rotate(grad_q_rot, cos_tab, -sin_tab).reshape(batch_size, seq_loc, kv_heads, group_q, head_dim)
        grad_k = rotate(grad_k_rot, cos_tab, -sin_tab)
        grad_qkv = jnp.concatenate([grad_q, grad_k[:, :, :, None, :], grad_v[:, :, :, None, :]], axis=3)

        grad_w_qkv = jnp.einsum('bsd,bsgjh->dgjh', h_norm, grad_qkv, preferred_element_type=jnp.float32)
        grad_h = jnp.einsum('bsgjh,dgjh->bsd', grad_qkv, w_qkv, preferred_element_type=jnp.float32).astype(jnp.bfloat16)
        grad_x, grad_gain, grad_bias = ln_back(grad_h)
        grad_w_qkv, grad_w_out, grad_gain, grad_bias = lax.psum((grad_w_qkv, grad_w_out, grad_gain, grad_bias), 'sp')
        return attn_out, grad_x, grad_w_qkv, grad_w_out, grad_gain, grad_bias

    return jax.shard_map(per_device, mesh=mesh, in_specs=(seq_spec, seq_spec, P(), P(), P(), P(), P('sp')), out_specs=(seq_spec, seq_spec, P(), P(), P(), P()), check_vma=False)
```

profile of v0, /device:TPU:0, one launch (start us, length us, event | category | flops | bytes accessed | tf_op | source)
XLA Modules:
  0.0 2130.8 jit_solution(14770851435323387705)
XLA Ops:
  14.8 31.2 %fusion.49 = bf16[8,64,8,6,128]{4,1,3,2,0:T(8,128)(2,1)S(1)} fusion(bf16[4096,8,6,128]{3,1,2,0:T(8,128)(2,1)} %param.9, bf16[8,64,4096]{2,1,0:T(8,128)(2,1)S(1)} %copy-done, f32[4096]{0:T(1024)S(1)} %copy-done.24, f32[4096]{0:T(1024)S(1)} %copy-done.13, f32[8,64]{1,0:T(8,128)S(1)} %fusion.71, f32[8,64]{1,0:T(8,128)S(1)} %broadcast_multiply_fusion), kind=kOutput, calls=%fused_computation.72 | convolution fusion | flops 25785532416 | bytes 60854272 | tf_op jit(solution)/shard_map/bsd,dgjh->bsgjh/dot_general | solution.py:54
  58.7 25.3 %all-to-all-done = bf16[8,64,16,128]{3,1,0,2:T(8,128)(2,1)} async-done(((bf16[8,64,16,128]{3,1,0,2:T(8,128)(2,1)}), bf16[8,64,16,128]{3,1,0,2:T(8,128)(2,1)}, u32[]{:S(2)}, u32[]{:S(2)}) %all-to-all-start) | async-done | bytes 2097184 | tf_op jit(solution)/shard_map/all_to_all | solution.py:61
  101.8 15.9 all-to-all-done.2
  121.7 22.7 %fusion.58 = bf16[8,8,32,8,128]{4,3,2,1,0:T(8,128)(2,1)S(1)} fusion(bf16[8,64,4096]{2,1,0:T(8,128)(2,1)} %param.8, bf16[4096,4096]{1,0:T(8,128)(2,1)} %param.10), kind=kOutput, calls=%fused_computation.73 | convolution fusion | flops 17181966336 | bytes 41943040 | tf_op jit(solution)/shard_map/bsd,cd->bsc/dot_general | solution.py:72
  147.7 27.5 %all-to-all-done.1 = bf16[8,64,32,128]{3,1,0,2:T(8,128)(2,1)} async-done(((bf16[8,64,32,128]{3,1,0,2:T(8,128)(2,1)}), bf16[8,64,32,128]{3,1,0,2:T(8,128)(2,1)}, u32[]{:S(2)}, u32[]{:S(2)}) %all-to-all-start.1) | async-done | bytes 4194336 | tf_op jit(solution)/shard_map/all_to_all | solution.py:59
  183.8 6.3 copy.99
  190.1 43.4 %all-to-all-done.4 = bf16[8,64,32,128]{3,1,0,2:T(8,128)(2,1)} async-done(((bf16[8,64,32,128]{3,1,0,2:T(8,128)(2,1)}), bf16[8,64,32,128]{3,1,0,2:T(8,128)(2,1)}, u32[]{:S(2)}, u32[]{:S(2)}) %all-to-all-start.4) | async-done | bytes 4194336 | tf_op jit(solution)/shard_map/all_to_all | solution.py:73
  233.5 5.6 copy.108
  239.1 31.5 %fusion.80 = (f32[8,1024,2]{1,2,0:T(2,128)S(1)}, f32[8,1024,2,1024]{1,3,2,0:T(8,128)}) fusion(pred[1024,1024]{0,1:T(8,128)(4,1)S(1)} %iota_compare_fusion, bf16[8,1024,2,128]{3,1,2,0:T(8,128)(2,1)} %bitcast.176, bf16[8,1024,128,1]{2,1,3,0:T(8,128)(2,1)} %bitcast.180), kind=kOutput, calls=%fused_computation.105 | convolution fusion | flops 4362077184 | bytes 74514432 | tf_op jit(solution)/shard_map/sub | solution.py:64
  270.6 25.9 %fusion.63 = bf16[8,1024,1,128]{1,3,0,2:T(8,128)(2,1)} fusion(bf16[8,1024,2,128]{3,1,2,0:T(8,128)(2,1)} %bitcast.161, f32[8,1024,2,1024]{1,3,2,0:T(8,128)} %get-tuple-element.56, f32[8,1024,2]{1,2,0:T(2,128)S(1)} %get-tuple-element.55), kind=kOutput, calls=%fused_computation.78 | convolution fusion | flops 4329570304 | bytes 73465856 | tf_op jit(solution)/shard_map/bgqjk,bqgjh->bkgh/dot_general | solution.py:75
  305.3 15.9 convolution_convert_fusion
  321.2 64.8 %fusion.66 = bf16[8,1024,1,128]{1,3,0,2:T(8,128)(2,1)S(1)} fusion(bf16[8,1024,2,128]{3,1,2,0:T(8,128)(2,1)} %bitcast.177, bf16[8,1024,2,1024]{1,3,2,0:T(8,128)(2,1)} %convolution_convert_fusion, f32[8,1024,2,1024]{1,3,2,0:T(8,128)} %get-tuple-element.56, f32[8,1024,2]{1,2,0:T(2,128)S(1)} %get-tuple-element.55), kind=kOutput, calls=%fused_computation.79 | convolution fusion | flops 4447028224 | bytes 107020288 | tf_op jit(solution)/shard_map/bgqjk,bqgjh->bkgh/dot_general | solution.py:80
  392.8 65.0 %convert_bitcast_fusion.1 = bf16[8,1024,2,128]{1,3,2,0:T(8,128)(2,1)} fusion(bf16[8,1024,128,1]{2,1,3,0:T(8,128)(2,1)} %bitcast.181, bf16[8,1024,2,1024]{1,3,2,0:T(8,128)(2,1)} %convolution_convert_fusion, f32[8,1024,2,1024]{1,3,2,0:T(8,128)} %get-tuple-element.56, f32[8,1024,2]{1,2,0:T(2,128)S(1)} %get-tuple-element.55), kind=kOutput, calls=%fused_computation.69 | convolution fusion | flops 4448076800 | bytes 107020288 | tf_op jit(solution)/shard_map/bgqjk,bkgh->bqgjh/dot_general | solution.py:79
  457.8 11.1 copy.111
  484.8 41.5 %all-to-all-done.5 = bf16[8,1024,2,128]{3,2,0,1:T(2,128)(2,1)} async-done(((bf16[8,1024,2,128]{3,2,0,1:T(2,128)(2,1)}), bf16[8,1024,2,128]{3,2,0,1:T(2,128)(2,1)}, u32[]{:S(2)}, u32[]{:S(2)}) %all-to-all-start.5) | async-done | bytes 4194336 | tf_op jit(solution)/shard_map/all_to_all | solution.py:82
  539.1 40.7 %convolution_bitcast_fusion.1 = f32[4096,8,6,128]{3,0,2,1:T(8,128)} fusion(bf16[8,64,8,1,128]{4,1,3,0,2:T(8,128)(2,1)S(1)} %bitcast.179, bf16[8,64,4096]{2,1,0:T(8,128)(2,1)S(1)} %copy-done.1, f32[4096]{0:T(1024)S(1)} %copy-done.25, f32[4096]{0:T(1024)S(1)} %copy-done.14, f32[8,64]{1,0:T(8,128)S(1)} %copy-done.20, f32[8,64]{1,0:T(8,128)S(1)} %copy-done.17, ...), kind=kOutput, calls=%fused_computation.17 | convolution fusion | flops 25803358208 | bytes 111185920 | tf_op jit(solution)/shard_map/bsd,bsgjh->dgjh/dot_general | solution.py:91
  581.4 24.7 %convert_bitcast_fusion.2 = bf16[8,1024,2,128]{1,3,2,0:T(8,128)(2,1)} fusion(bf16[8,1024,128,1]{2,1,3,0:T(8,128)(2,1)S(1)} %bitcast.170, f32[8,1024,2,1024]{1,3,2,0:T(8,128)} %get-tuple-element.56, f32[8,1024,2]{1,2,0:T(2,128)S(1)} %copy-done.28), kind=kOutput, calls=%fused_computation.70 | convolution fusion | flops 4330618880 | bytes 73465856 | tf_op jit(solution)/shard_map/bgqjk,bkgh->bqgjh/dot_general | solution.py:66
  606.1 11.1 copy.104
  617.3 88.3 %all_to_all.114 = bf16[8,1024,2,128]{3,2,0,1:T(2,128)(2,1)S(1)} all-to-all(bf16[8,1024,2,128]{3,2,0,1:T(2,128)(2,1)} %copy.104), channel_id=1, replica_groups=mesh['sp'=16] {'sp'}, dimensions={1} | all-to-all | bytes 8388608 | tf_op jit(solution)/shard_map/all_to_all | solution.py:67
  706.6 6.3 copy.106
  713.0 7.8 reshape.289
  720.7 30.9 %convolution_bitcast_fusion = f32[4096,4096]{1,0:T(8,128)} fusion(bf16[8,64,4096]{2,1,0:T(8,128)(2,1)} %reshape.289, bf16[8,64,4096]{2,1,0:T(8,128)(2,1)} %param.8), kind=kOutput, calls=%fused_computation.16 | convolution fusion | flops 17179869184 | bytes 75497472 | tf_op jit(solution)/shard_map/bsc,bsd->cd/dot_general | solution.py:71
  751.7 7.0 pad_maximum_fusion.4.clone.4
  758.7 52.2 %convert_reduce_fusion = (f32[4096]{0:T(1024)S(1)}, f32[8,64]{1,0:T(8,128)S(1)}, bf16[8,64,4096]{2,1,0:T(8,128)(2,1)}) fusion(f32[4096]{0:T(1024)S(1)} %copy-done.15, f32[8,64]{1,0:T(8,128)S(1)} %copy-done.18, bf16[8,64,4096]{2,1,0:T(8,128)(2,1)S(1)} %copy-done.2, bf16[4096,8,6,128,1]{3,1,2,0,4:T(8,128)(2,1)} %bitcast.182, ...), kind=kOutput, calls=%fused_computation.34 | convolution fusion | flops 25786576896 | bytes 65048576 | tf_op jit(solution)/shard_map/bsgjh,dgjh->bsd/dot_general | solution.py:92
  810.9 6.1 fusion.35
  817.0 32.3 %all-reduce = (f32[4096]{0:T(1024)}, f32[4096]{0:T(1024)}) all-reduce(f32[4096]{0:T(1024)S(1)} %get-tuple-element.36, f32[4096]{0:T(1024)S(1)} %get-tuple-element.38), channel_id=1, replica_groups=mesh['sp'=16] {'sp'}, use_global_device_ids=true, to_apply=%region_12.13 | all-reduce | flops 8192 | bytes 65536 | tf_op jit(solution)/shard_map/psum | solution.py:94
  849.4 7.3 add_convert_fusion
  856.7 22.7 %fusion.40 = bf16[8,64,4096]{2,1,0:T(8,128)(2,1)} fusion(bf16[8,64,4096]{2,1,0:T(8,128)(2,1)S(1)} %copy-done.6, bf16[4096,4096]{1,0:T(8,128)(2,1)} %param.10), kind=kOutput, calls=%fused_computation.59 | convolution fusion | flops 17181966336 | bytes 41943040 | tf_op jit(solution)/shard_map/bsc,cd->bsd/dot_general | solution.py:69
  879.4 607.2 %all-reduce.4.cloned.1.call-done = f32[4096,8,6,128]{3,0,2,1:T(8,128)} async-done(((f32[4096,8,6,128]{3,0,2,1:T(8,128)}), f32[4096,8,6,128]{3,0,2,1:T(8,128)}) %all-reduce.4.cloned.1.call-update) | async-done | bytes 100663312 | tf_op jit(solution)/shard_map/psum | solution.py:94
  1486.5 82.8 %copy.128 = f32[4096,8,6,128]{3,1,2,0:T(8,128)} copy(f32[4096,8,6,128]{3,0,2,1:T(8,128)} %all-reduce.4.cloned.1.call-done) | data formatting | bytes 201326592
  1569.3 510.1 %all-reduce.6.cloned.1.call-done = f32[4096,4096]{1,0:T(8,128)} async-done(((f32[4096,4096]{1,0:T(8,128)}), f32[4096,4096]{1,0:T(8,128)}) %all-reduce.6.cloned.1.call-update) | async-done | bytes 67108880 | tf_op jit(solution)/shard_map/psum | solution.py:94
  2079.4 44.1 %copy.191 = f32[4096,4096]{1,0:T(8,128)} copy(f32[4096,4096]{1,0:T(8,128)} %all-reduce.6.cloned.1.call-done) | data formatting | bytes 134217728
  (112 shorter events, 100.7 us)
Async XLA Ops:
  7.2 7.6 copy-start
  7.2 7.6 copy-start.24
  7.2 7.6 copy-start.13
  10.2 4.0 copy-start.16
  48.7 7.7 copy-start.26
  51.1 32.9 %all-to-all-start = ((bf16[8,64,16,128]{3,1,0,2:T(8,128)(2,1)}), bf16[8,64,16,128]{3,1,0,2:T(8,128)(2,1)}, u32[]{:S(2)}, u32[]{:S(2)}) async-start(bf16[8,64,16,128]{3,1,0,2:T(8,128)(2,1)} %bitcast.172), calls=%async_computation | async-start | bytes 4194304 | tf_op jit(solution)/shard_map/all_to_all | solution.py:61
  57.3 36.1 %copy-start.10 = (f32[64,64]{1,0:T(8,128)}, f32[64,64]{1,0:T(8,128)S(1)}, u32[]{:S(2)}) copy-start(f32[64,64]{1,0:T(8,128)S(1)} %get-tuple-element.54) | copy-start | bytes 49156
  86.0 31.7 %all-to-all-start.2 = ((bf16[8,64,16,128]{3,1,0,2:T(8,128)(2,1)}), bf16[8,64,16,128]{3,1,0,2:T(8,128)(2,1)S(1)}, u32[]{:S(2)}, u32[]{:S(2)}) async-start(bf16[8,64,16,128]{3,1,0,2:T(8,128)(2,1)} %bitcast.173), calls=%async_computation.2 | async-start | bytes 4194304 | tf_op jit(solution)/shard_map/all_to_all | solution.py:60
  117.8 57.4 %all-to-all-start.1 = ((bf16[8,64,32,128]{3,1,0,2:T(8,128)(2,1)}), bf16[8,64,32,128]{3,1,0,2:T(8,128)(2,1)}, u32[]{:S(2)}, u32[]{:S(2)}) async-start(bf16[8,64,32,128]{3,1,0,2:T(8,128)(2,1)} %copy.98), calls=%async_computation.1 | async-start | bytes 8388608 | tf_op jit(solution)/shard_map/all_to_all | solution.py:59
  175.2 58.3 %all-to-all-start.4 = ((bf16[8,64,32,128]{3,1,0,2:T(8,128)(2,1)}), bf16[8,64,32,128]{3,1,0,2:T(8,128)(2,1)}, u32[]{:S(2)}, u32[]{:S(2)}) async-start(bf16[8,64,32,128]{3,1,0,2:T(8,128)(2,1)} %bitcast.165), calls=%async_computation.4 | async-start | bytes 8388608 | tf_op jit(solution)/shard_map/all_to_all | solution.py:73
  183.8 121.5 %copy-start.4 = (bf16[8,64,16,128]{3,1,2,0:T(8,128)(2,1)}, bf16[8,64,16,128]{3,1,2,0:T(8,128)(2,1)S(1)}, u32[]{:S(2)}) copy-start(bf16[8,64,16,128]{3,1,2,0:T(8,128)(2,1)S(1)} %copy.97) | copy-start | bytes 6291460
  270.6 122.2 %copy-start.27 = (f32[8,1024,2]{1,2,0:T(2,128)}, f32[8,1024,2]{1,2,0:T(2,128)S(1)}, u32[]{:S(2)}) copy-start(f32[8,1024,2]{1,2,0:T(2,128)S(1)} %get-tuple-element.55) | copy-start | bytes 196612
  300.7 88.2 %all-to-all-start.7 = ((bf16[8,1024,1,128]{3,0,2,1:T(8,128)(2,1)}), bf16[8,1024,1,128]{3,0,2,1:T(8,128)(2,1)}, u32[]{:S(2)}, u32[]{:S(2)}) async-start(bf16[8,1024,1,128]{3,0,2,1:T(8,128)(2,1)} %copy.122), calls=%async_computation.7 | async-start | bytes 4194304 | tf_op jit(solution)/shard_map/all_to_all | solution.py:84
  388.9 80.0 %all-to-all-start.6 = ((bf16[8,1024,1,128]{3,0,2,1:T(8,128)(2,1)}), bf16[8,1024,1,128]{3,0,2,1:T(8,128)(2,1)S(1)}, u32[]{:S(2)}, u32[]{:S(2)}) async-start(bf16[8,1024,1,128]{3,0,2,1:T(8,128)(2,1)} %copy.118), calls=%async_computation.6 | async-start | bytes 4194304 | tf_op jit(solution)/shard_map/all_to_all | solution.py:83
  468.9 57.4 %all-to-all-start.5 = ((bf16[8,1024,2,128]{3,2,0,1:T(2,128)(2,1)}), bf16[8,1024,2,128]{3,2,0,1:T(2,128)(2,1)}, u32[]{:S(2)}, u32[]{:S(2)}) async-start(bf16[8,1024,2,128]{3,2,0,1:T(2,128)(2,1)} %copy.111), calls=%async_computation.5 | async-start | bytes 8388608 | tf_op jit(solution)/shard_map/all_to_all | solution.py:82
  472.8 1013.7 %all-reduce.4.cloned.1.call-start = ((), (), s32[]{:S(2)}) async-start(), calls=%async_computation.8 | async-start | bytes 201326592 | tf_op jit(solution)/shard_map/psum | solution.py:94
  476.4 7.4 copy-start.11
  476.4 7.5 copy-start.12
  484.7 54.4 %copy-start.7 = (bf16[8,64,8,1,64]{4,1,2,0,3:T(8,128)(2,1)}, bf16[8,64,8,1,64]{4,1,2,0,3:T(8,128)(2,1)S(1)}, u32[]{:S(2)}) copy-start(bf16[8,64,8,1,64]{4,1,2,0,3:T(8,128)(2,1)S(1)} %get-tuple-element.48) | copy-start | bytes 1572868
  484.7 54.3 %copy-start.8 = (bf16[8,64,8,1,64]{4,1,2,0,3:T(8,128)(2,1)}, bf16[8,64,8,1,64]{4,1,2,0,3:T(8,128)(2,1)S(1)}, u32[]{:S(2)}) copy-start(bf16[8,64,8,1,64]{4,1,2,0,3:T(8,128)(2,1)S(1)} %get-tuple-element.49) | copy-start | bytes 1572868
  535.1 3.9 copy-start.1
  535.2 3.9 copy-start.9
  535.2 3.9 copy-start.14
  535.2 3.9 copy-start.17
  535.2 3.9 copy-start.20
  579.8 1499.6 %all-reduce.6.cloned.1.call-start = ((), (), s32[]{:S(2)}) async-start(), calls=%async_computation.9 | async-start | bytes 134217728 | tf_op jit(solution)/shard_map/psum | solution.py:94
  751.7 7.0 copy-start.2
  751.7 7.0 copy-start.15
  751.7 7.0 copy-start.18
  758.7 52.2 %copy-start.23 = (f32[8,64]{1,0:T(8,128)S(1)}, f32[8,64]{1,0:T(8,128)}, u32[]{:S(2)}) copy-start(f32[8,64]{1,0:T(8,128)} %copy-done.22) | copy-start | bytes 6148
  758.7 52.2 %copy-start.21 = (f32[8,64]{1,0:T(8,128)S(1)}, f32[8,64]{1,0:T(8,128)}, u32[]{:S(2)}) copy-start(f32[8,64]{1,0:T(8,128)} %copy-done.19) | copy-start | bytes 6148
  849.4 7.3 copy-start.6
  (7 other events, 13.2 us)
Sparse Core Ops, SparseCore 0:
  580.0 906.5 all-reduce.3
  1492.8 586.5 all-reduce.5
where the time goes:
time: 2140 us; the launch traced here: 2130 us
  waiting for transfers between devices  1270 us (59%)
  matrix products  428 us (20%)
  local copies, waits for them, and re-layouts  216 us (10%)
  blocking collectives  121 us (6%)
  other arithmetic  49.5 us (2%)
  starting transfers between devices  31.1 us (1%)
    psum x2, waiting for transfers between devices, per_device(): lax.psum((grad_w_qkv, grad_w_out, grad_gain, grad_bias), 'sp')  1120 us
    unnamed x60, local copies, waits for them, and re-layouts  132 us
    all_to_all x1, blocking collectives, per_device(): lax.all_to_all(head_ctx.reshape(batch_size, seq_all, q_local, head_dim),...  88.3 us
    dot_general x1, matrix products, per_device(): jnp.einsum('bgqjk,bkgh->bqgjh', grad_scores, k_heads, preferred_element_t...  65 us
    dot_general x1, matrix products, per_device(): jnp.einsum('bgqjk,bqgjh->bkgh', grad_scores, q_heads, preferred_element_t...  64.8 us
    dot_general x1, matrix products, per_device(): jnp.einsum('bsgjh,dgjh->bsd', grad_qkv, w_qkv, preferred_element_type=jnp...  52.2 us
    all_to_all x1, waiting for transfers between devices, per_device(): lax.all_to_all(grad_ctx.reshape(batch_size, seq_loc, num_heads, head_dim)...  43.4 us
  transfers between devices with their start and end apart: 9, of which 7 were waited for; matrix products, arithmetic and copies ran while one was open for 22% of the time, Pallas kernels for 0%

commit v1 on v0

v1 whole, which is shorter than its diff:
```python
import functools

import jax
import jax.numpy as jnp
from jax import lax
from jax.experimental import pallas as pl
from jax.experimental.pallas import tpu as pltpu
from jax.sharding import PartitionSpec as P


LN_EPS = 1e-5
ROPE_BASE = 10000.0
F32 = jnp.float32
BF16 = jnp.bfloat16
QB = 256


def layer_norm(x_rows, ln_gain, ln_bias):
    x_f32 = x_rows.astype(F32)
    centered = x_f32 - jnp.mean(x_f32, axis=-1, keepdims=True)
    variance = jnp.mean(centered * centered, axis=-1, keepdims=True)
    return (centered * lax.rsqrt(variance + LN_EPS) * ln_gain + ln_bias).astype(BF16)


def rope_tables(positions, head_dim):
    exponents = jnp.arange(head_dim // 2, dtype=F32) * (2.0 / head_dim)
    inv_freq = jnp.power(ROPE_BASE, -exponents)
    angles = positions.astype(F32)[:, None] * inv_freq[None, :]
    cos_half, sin_half = jnp.cos(angles), jnp.sin(angles)
    return jnp.concatenate([cos_half, cos_half], axis=-1), jnp.concatenate([-sin_half, sin_half], axis=-1)


def rotate(t_in, cos_full, sin_signed):
    t_f32 = t_in.astype(F32)
    half_dim = t_in.shape[-1] // 2
    swapped = jnp.concatenate([t_f32[..., half_dim:], t_f32[..., :half_dim]], axis=-1)
    return (t_f32 * cos_full + swapped * sin_signed).astype(BF16)


def rotate_rows(t_in, cos_full, sin_signed):
    t_f32 = t_in.astype(F32)
    swapped = pltpu.roll(t_f32, t_in.shape[-1] // 2, 1)
    return (t_f32 * cos_full + swapped * sin_signed).astype(BF16)


def dot(a, b, dims):
    return lax.dot_general(a, b, (dims, ((), ())), preferred_element_type=F32)


def masked_scores(k_rot, q_rot, block, scale):
    keys = (block + 1) * QB
    scores = dot(k_rot[:keys], q_rot[block * QB:keys], ((1,), (1,))) * scale
    key_id = lax.broadcasted_iota(jnp.int32, (QB, QB), 0)
    query_id = lax.broadcasted_iota(jnp.int32, (QB, QB), 1)
    diag = jnp.where(key_id <= query_id, scores[block * QB:], -jnp.inf)
    return jnp.concatenate([scores[:block * QB], diag], axis=0) if block else diag


def attn_fwd_kernel(q_ref, k_ref, v_ref, cos_ref, sin_ref, ctx_ref, qr_ref, kr_ref, max_ref, sum_ref, turn_ref, *, scale):
    chunks, _, rows, head_dim = q_ref.shape
    seq = chunks * rows
    cos_full, sin_signed = cos_ref[...], sin_ref[...]
    q_rot = rotate_rows(q_ref[...].reshape(seq, head_dim), cos_full, sin_signed)
    k_rot = rotate_rows(k_ref[...].reshape(seq, head_dim), cos_full, sin_signed)
    qr_ref[...] = q_rot.reshape(q_ref.shape)
    kr_ref[...] = k_rot.reshape(q_ref.shape)
    v_t = v_ref[...].reshape(seq, head_dim).T
    per = QB // rows
    for block in range(seq // QB):
        keys = (block + 1) * QB
        scores = masked_scores(k_rot, q_rot, block, scale)
        row_max = jnp.max(scores, axis=0, keepdims=True)
        expd = jnp.exp(scores - row_max)
        row_sum = jnp.sum(expd, axis=0, keepdims=True)
        probs = (expd * (1.0 / row_sum)).astype(BF16)
        turn_ref[...] = dot(v_t[:, :keys], probs, ((1,), (0,)))
        ctx = turn_ref[...].T.astype(BF16)
        ctx_ref[block * per:(block + 1) * per] = ctx.reshape(per, 1, rows, head_dim)
        max_ref[0, 0, :, block * QB:keys] = row_max
        sum_ref[0, 0, :, block * QB:keys] = row_sum


def attn_bwd_kernel(q_ref, k_ref, v_ref, g_ref, cos_ref, sin_ref, max_ref, sum_ref, gq_ref, gk_ref, gv_ref, gk_acc, gv_acc, turn_ref, *, scale):
    chunks, _, rows, head_dim = q_ref.shape
    seq = chunks * rows
    head = pl.program_id(1)
    q_rot = q_ref[...].reshape(seq, head_dim)
    k_rot = k_ref[...].reshape(seq, head_dim)
    v_val = v_ref[...].reshape(seq, head_dim)
    g_val = g_ref[...].reshape(seq, head_dim)
    k_t = k_rot.T
    per = QB // rows

    @pl.when(head == 0)
    def _():
        gk_acc[...] = jnp.zeros_like(gk_acc)
        gv_acc[...] = jnp.zeros_like(gv_acc)

    for block in range(seq // QB):
        keys = (block + 1) * QB
        span = slice(block * QB, keys)
        scores = masked_scores(k_rot, q_rot, block, scale)
        probs = jnp.exp(scores - max_ref[0, 0, :, span]) * (1.0 / sum_ref[0, 0, :, span])
        g_blk = g_val[span]
        gv_acc[:keys] += dot(probs.astype(BF16), g_blk, ((1,), (0,)))
        grad_probs = dot(v_val[:keys], g_blk, ((1,), (1,))).astype(BF16).astype(F32)
        row_dot = jnp.sum(grad_probs * probs, axis=0, keepdims=True)
        grad_scores = (probs * (grad_probs - row_dot) * scale).astype(BF16)
        gk_acc[:keys] += dot(grad_scores, q_rot[span], ((1,), (0,)))
        turn_ref[...] = dot(k_t[:, :keys], grad_scores, ((1,), (0,)))
        gq = rotate_rows(turn_ref[...].T.astype(BF16), cos_ref[span], -sin_ref[span])
        gq_ref[block * per:(block + 1) * per] = gq.reshape(per, 1, rows, head_dim)

    @pl.when(head == pl.num_programs(1) - 1)
    def _():
        gk_ref[...] = gk_acc[...].astype(BF16).reshape(gk_ref.shape)
        gv_ref[...] = gv_acc[...].astype(BF16).reshape(gv_ref.shape)


def attn_specs(chunks, rows, head_dim):
    seq = chunks * rows
    blk = (chunks, 1, rows, head_dim)
    per_head = pl.BlockSpec(blk, lambda b, h: (0, b, 0, h))
    col = lambda c: pl.BlockSpec(blk, lambda b, h: (0, b, 0, c))
    table = pl.BlockSpec((seq, head_dim), lambda b, h: (0, 0))
    stat = pl.BlockSpec((1, 1, 1, seq), lambda b, h: (b, h, 0, 0))
    return per_head, col, table, stat


def attn_params(batch, heads, seq, head_dim, dots, name):
    flops = batch * heads * dots * seq * seq * head_dim
    return dict(
        cost_estimate=pl.CostEstimate(flops=flops, bytes_accessed=batch * seq * head_dim * 20, transcendentals=batch * heads * seq * seq // 2),
        compiler_params=pltpu.CompilerParams(dimension_semantics=("arbitrary", "arbitrary"), vmem_limit_bytes=48 * 2**20),
        name=name,
    )


def attn_fwd(qkv, cos_full, sin_signed, heads, scale):
    chunks, batch, rows, width = qkv.shape
    head_dim = width // (heads + 2)
    seq = chunks * rows
    per_head, col, table, stat = attn_specs(chunks, rows, head_dim)
    out = lambda n: jax.ShapeDtypeStruct((chunks, batch, rows, n * head_dim), BF16)
    stats = jax.ShapeDtypeStruct((batch, heads, 1, seq), F32)
    return pl.pallas_call(
        functools.partial(attn_fwd_kernel, scale=scale),
        grid=(batch, heads),
        in_specs=[per_head, col(heads), col(heads + 1), table, table],
        out_specs=[per_head, per_head, col(0), stat, stat],
        out_shape=[out(heads), out(heads), out(1), stats, stats],
        scratch_shapes=[pltpu.VMEM((head_dim, QB), F32)],
        **attn_params(batch, heads, seq, head_dim, 2, "attn_fwd"),
    )(qkv, qkv, qkv, cos_full, sin_signed)


def attn_bwd(q_rot, k_rot, qkv, grad_ctx, cos_full, sin_signed, row_max, row_sum, heads, scale):
    chunks, batch, rows, width = qkv.shape
    head_dim = width // (heads + 2)
    seq = chunks * rows
    per_head, col, table, stat = attn_specs(chunks, rows, head_dim)
    out = lambda n: jax.ShapeDtypeStruct((chunks, batch, rows, n * head_dim), BF16)
    return pl.pallas_call(
        functools.partial(attn_bwd_kernel, scale=scale),
        grid=(batch, heads),
        in_specs=[per_head, col(0), col(heads + 1), per_head, table, table, stat, stat],
        out_specs=[per_head, col(0), col(0)],
        out_shape=[out(heads), out(1), out(1)],
        scratch_shapes=[pltpu.VMEM((seq, head_dim), F32), pltpu.VMEM((seq, head_dim), F32), pltpu.VMEM((head_dim, QB), F32)],
        **attn_params(batch, heads, seq, head_dim, 5, "attn_bwd"),
    )(q_rot, k_rot, qkv, grad_ctx, cos_full, sin_signed, row_max, row_sum)


def device_slots(device, group_q):
    core, half = device % 2, group_q // 2
    return [core * half + n for n in range(half)] + [group_q + core]


def place_kernel(part_ref, old_ref, out_ref, *, kv_heads, group_q):
    del old_ref
    devices, rows, _ = part_ref.shape
    head_dim = out_ref.shape[1]
    slots = group_q + 2
    for device in range(devices):
        for n, slot in enumerate(device_slots(device, group_q)):
            out_ref[pl.ds(slot * kv_heads + device // 2, rows, slots * kv_heads), :] = part_ref[device, :, n * head_dim:(n + 1) * head_dim]


def split_kernel(w_ref, dev_ref, wide_ref, *, kv_heads, group_q):
    devices, rows, _ = dev_ref.shape
    head_dim = w_ref.shape[1]
    slots = group_q + 2
    wide_ref[...] = w_ref[...].astype(F32)
    for device in range(devices):
        for n, slot in enumerate(device_slots(device, group_q)):
            picked = wide_ref[pl.ds(slot * kv_heads + device // 2, rows, slots * kv_heads), :]
            dev_ref[device, :, n * head_dim:(n + 1) * head_dim] = picked.astype(BF16)


def split(w_flat, width, devices, kv_heads, group_q):
    slots, head_dim = (group_q + 2) * kv_heads, w_flat.shape[1]
    blk = 64
    cols = (group_q // 2 + 1) * head_dim
    return pl.pallas_call(
        functools.partial(split_kernel, kv_heads=kv_heads, group_q=group_q),
        grid=(width // blk,),
        in_specs=[pl.BlockSpec((blk * slots, head_dim), lambda i: (i, 0))],
        out_specs=pl.BlockSpec((devices, blk, cols), lambda i: (0, i, 0)),
        out_shape=jax.ShapeDtypeStruct((devices, width, cols), BF16),
        scratch_shapes=[pltpu.VMEM((blk * slots, head_dim), F32)],
        cost_estimate=pl.CostEstimate(flops=width * slots * head_dim * 2000, bytes_accessed=4 * width * slots * head_dim, transcendentals=0),
        compiler_params=pltpu.CompilerParams(dimension_semantics=("arbitrary",), vmem_limit_bytes=48 * 2**20),
        name="split",
    )(w_flat)


def place(part, old, index, pieces, kv_heads, group_q):
    devices, rows, width = part.shape
    head_dim = width // (group_q // 2 + 1)
    slots = (group_q + 2) * kv_heads
    blk = 64
    steps = rows // blk
    out_shape = jax.ShapeDtypeStruct((pieces * rows * slots, head_dim), F32)
    kernel = functools.partial(place_kernel, kv_heads=kv_heads, group_q=group_q)
    in_specs = [pl.BlockSpec((devices, blk, width), lambda i: (0, i, 0))]
    args = [part]
    alias = {}
    if old is None:
        kernel_fn = lambda part_ref, out_ref: kernel(part_ref, None, out_ref)
    else:
        kernel_fn = kernel
        in_specs.append(pl.BlockSpec(memory_space=pl.ANY))
        args.append(old)
        alias = {1: 0}
    return pl.pallas_call(
        kernel_fn,
        grid=(steps,),
        in_specs=in_specs,
        out_specs=pl.BlockSpec((blk * slots, head_dim), lambda i: (index * steps + i, 0)),
        out_shape=out_shape,
        input_output_aliases=alias,
        cost_estimate=pl.CostEstimate(flops=rows * slots * head_dim * 2000, bytes_accessed=2 * 4 * rows * slots * head_dim, transcendentals=0),
        compiler_params=pltpu.CompilerParams(dimension_semantics=("arbitrary",), vmem_limit_bytes=48 * 2**20),
        name="place",
    )(*args)


def copy(array):
    rows, width = array.shape
    blk = pl.BlockSpec((256, width), lambda i: (i, 0))

    def kernel(in_ref, out_ref):
        out_ref[...] = in_ref[...]

    return pl.pallas_call(
        kernel,
        grid=(rows // 256,),
        in_specs=[blk],
        out_specs=blk,
        out_shape=jax.ShapeDtypeStruct(array.shape, array.dtype),
        cost_estimate=pl.CostEstimate(flops=rows * width * 2000, bytes_accessed=8 * rows * width, transcendentals=0),
        compiler_params=pltpu.CompilerParams(dimension_semantics=("arbitrary",), vmem_limit_bytes=48 * 2**20),
    )(array)


def solution(mesh):
    sp_size = mesh.shape['sp']
    seq_spec = P(None, 'sp', None)
    pieces = 4

    def per_device(x_loc, dy_loc, w_qkv, w_out, ln_gain, ln_bias, pos_loc):
        batch, seq_loc, width = x_loc.shape
        kv_heads, head_dim = w_qkv.shape[1], w_qkv.shape[3]
        group_q = w_qkv.shape[2] - 2
        heads = kv_heads * group_q // sp_size
        scale = head_dim ** -0.5
        me = lax.axis_index('sp')
        group, core = me // 2, me % 2
        own_w = heads * head_dim

        h_norm, ln_back = jax.vjp(layer_norm, x_loc, ln_gain, ln_bias)
        h_all = lax.all_gather(h_norm, 'sp')
        dy_all = lax.all_gather(dy_loc, 'sp')
        pos_all = lax.all_gather(pos_loc, 'sp', tiled=True)
        cos_full, sin_signed = rope_tables(pos_all, head_dim)

        w_dev = split(w_qkv.transpose(0, 2, 1, 3).reshape(-1, head_dim), width, sp_size, kv_heads, group_q)
        pair = lax.dynamic_slice(w_dev, (2 * group, 0, own_w), (2, width, head_dim))
        w_own = jnp.concatenate([lax.dynamic_slice(w_dev, (me, 0, 0), (1, width, own_w))[0], pair[0], pair[1]], axis=-1)
        w_out_own = lax.dynamic_slice(w_out, (me * own_w, 0), (own_w, width))

        tokens = sp_size * batch * seq_loc
        by_chunk = lambda t: t.reshape(sp_size, batch, seq_loc, t.shape[-1])
        flat = lambda t: t.reshape(tokens, t.shape[-1])
        h_rows, dy_rows = flat(h_all), flat(dy_all)

        qkv = by_chunk(dot(h_rows, w_own, ((1,), (0,))).astype(BF16))
        ctx, q_rot, k_rot, row_max, row_sum = attn_fwd(qkv, cos_full, sin_signed, heads, scale)
        ctx_got = lax.all_to_all(ctx, 'sp', 0, 0)

        grad_w_out_own = dot(flat(ctx), dy_rows, ((0,), (0,)))
        grad_w_out = copy(lax.all_gather(grad_w_out_own, 'sp', tiled=True))

        grad_ctx = jnp.einsum('ibsd,cd->ibsc', dy_all, w_out_own, preferred_element_type=F32).astype(BF16)
        grad_ctx, grad_w_out_own = lax.optimization_barrier((grad_ctx, grad_w_out_own))
        grad_q, grad_k_part, grad_v_part = attn_bwd(q_rot, k_rot, qkv, grad_ctx, cos_full, sin_signed, row_max, row_sum, heads, scale)
        kept = jnp.where(core == 0, grad_k_part, grad_v_part)
        sent = jnp.where(core == 0, grad_v_part, grad_k_part)
        got = lax.ppermute(sent, 'sp', [(i, i ^ 1) for i in range(sp_size)])
        grad_kv = (kept.astype(F32) + got.astype(F32)).astype(BF16)
        pos_of = lambda table: table.reshape(sp_size, 1, seq_loc, head_dim)
        grad_kv = jnp.where(core == 0, rotate(grad_kv, pos_of(cos_full), pos_of(-sin_signed)), grad_kv)
        grad_own = jnp.concatenate([grad_q, grad_kv], axis=-1)
        grad_got = lax.all_to_all(grad_own, 'sp', 0, 0)

        rows = width // pieces
        grad_w_own = dot(h_rows, flat(grad_own), ((0,), (0,)))
        grad_w = None
        for n in range(pieces):
            part = lax.all_gather(grad_w_own[n * rows:(n + 1) * rows], 'sp')
            grad_w = place(part, grad_w, n, pieces, kv_heads, group_q)
        grad_w_qkv = grad_w.reshape(width, group_q + 2, kv_heads, head_dim).transpose(0, 2, 1, 3)

        attn_out = jnp.einsum('ibsc,icd->bsd', ctx_got, w_out.reshape(sp_size, own_w, width), preferred_element_type=F32).astype(BF16)
        grad_h = jnp.einsum('ibsc,idc->bsd', grad_got, w_dev, preferred_element_type=F32).astype(BF16)
        grad_x, grad_gain, grad_bias = ln_back(grad_h)
        grad_gain, grad_bias = lax.psum((grad_gain, grad_bias), 'sp')
        return attn_out, grad_x, grad_w_qkv, grad_w_out, grad_gain, grad_bias

    return jax.shard_map(per_device, mesh=mesh, in_specs=(seq_spec, seq_spec, P(), P(), P(), P(), P('sp')), out_specs=(seq_spec, seq_spec, P(), P(), P(), P()), check_vma=False)
```

time: 2140 us -> 1510 us (0.71)
  waiting for transfers between devices: 1270 us -> 830 us
  Pallas kernels: 0 us -> 317 us
  matrix products: 428 us -> 210 us
  local copies, waits for them, and re-layouts: 216 us -> 13.7 us
  blocking collectives: 121 us -> 71 us
  starting transfers between devices: 31.1 us -> 8.29 us
    psum x2 -> x0, waiting for transfers between devices: 1120 us -> none  [per_device(): lax.psum((grad_w_qkv, grad_w_out, grad_gain, grad_bias), 'sp')]
    all_gather x0 -> x7, waiting for transfers between devices: none -> 706 us  [the longest x1 217 us: per_device(): grad_w_out = copy(lax.all_gather(grad_w_out_own, 'sp', tiled=True))]
    pallas_call x0 -> x8, Pallas kernels: none -> 317 us  [the longest x4 111 us: place(): pl.pallas_call(kernel_fn, grid=(steps,), in_specs=in_specs, out_specs=pl....]
    dot_general x11 -> x6, matrix products: 397 us -> 210 us  [the longest x3 111 us: dot(): return lax.dot_general(a, b, (dims, ((), ())), preferred_element_type=F32)]
    unnamed x60 -> x46, local copies, waits for them, and re-layouts: 132 us -> 4.57 us
    all_to_all x1 -> x0, blocking collectives: 88.3 us -> none  [per_device(): lax.all_to_all(head_ctx.reshape(batch_size, seq_all, q_local, head_dim),...]
    unnamed x0 -> x1, blocking collectives: none -> 36.3 us
    reshape x4 -> x0, local copies, waits for them, and re-layouts: 33.3 us -> none  [the longest x1 11.1 us: per_device(): grad_q_heads.reshape(batch_size, seq_all, q_local, head_dim)]
  transfers between devices with their start and end apart: 9 -> 10, of which waited for: 7 -> 9; matrix products, arithmetic and copies ran while one was open for 22% -> 9% of each run, Pallas kernels for 0% -> 15%
where the time goes in v1:
time: 1510 us
  waiting for transfers between devices  830 us (55%)
  Pallas kernels  317 us (21%)
  matrix products  210 us (14%)
  blocking collectives  71 us (5%)
  other arithmetic  41.8 us (3%)
    all_gather x1, waiting for transfers between devices, per_device(): grad_w_out = copy(lax.all_gather(grad_w_out_own, 'sp', tiled=True))  217 us
    all_gather x4, waiting for transfers between devices, per_device(): part = lax.all_gather(grad_w_own[n * rows:(n + 1) * rows], 'sp')  196 us
    all_gather x1, waiting for transfers between devices, per_device(): dy_all = lax.all_gather(dy_loc, 'sp')  162 us
    all_gather x1, waiting for transfers between devices, per_device(): h_all = lax.all_gather(h_norm, 'sp')  132 us
    dot_general x3, matrix products, dot(): return lax.dot_general(a, b, (dims, ((), ())), preferred_element_type=F32)  111 us
    pallas_call x4, Pallas kernels, place(): pl.pallas_call(kernel_fn, grid=(steps,), in_specs=in_specs, out_specs=pl....  111 us
    pallas_call x1, Pallas kernels, split(): pl.pallas_call(functools.partial(split_kernel, kv_heads=kv_heads, group_q...  69.6 us
    all_to_all x1, waiting for transfers between devices, per_device(): grad_got = lax.all_to_all(grad_own, 'sp', 0, 0)  65.6 us
  transfers between devices with their start and end apart: 10, of which 9 were waited for; matrix products, arithmetic and copies ran while one was open for 9% of the time, Pallas kernels for 15%

profile of v1, /device:TPU:0, one launch (start us, length us, event | category | flops | bytes accessed | tf_op | source)
XLA Modules:
  0.0 1506.7 jit_solution(14931668792722958031)
XLA Ops:
  13.1 3.4 fusion.9
  17.6 36.3 %all-reduce = s32[1024]{0:T(1024)S(1)} all-reduce(s32[1024]{0:T(1024)S(1)} %dynamic-update-slice), channel_id=1, replica_groups=mesh['sp'=16] {'sp'}, use_global_device_ids=true, to_apply=%add | all-reduce | flops 1024 | bytes 8192
  56.2 69.6 %split.1 = bf16[16,4096,384]{2,1,0:T(8,128)(2,1)} custom-call(bf16[196608,128]{1,0:T(8,128)(2,1)} %bitcast.71), custom_call_target="tpu_custom_call" | custom-call | flops 50331648000 | bytes 100663296 | tf_op jit(solution)/shard_map/split/pallas_call | solution.py:204
  125.7 3.0 dynamic-slice_bitcast_fusion.2
  130.5 132.0 %all-gather.16.cloned.1.call-done = bf16[128,64,4096]{2,1,0:T(8,128)(2,1)} async-done(((bf16[8,64,4096]{2,1,0:T(8,128)(2,1)}), bf16[128,64,4096]{2,1,0:T(8,128)(2,1)}) %all-gather.16.cloned.1.call-update) | async-done | bytes 67108880 | tf_op jit(solution)/shard_map/all_gather | solution.py:282
  262.5 42.4 %convolution_convert_fusion = bf16[8192,512]{1,0:T(8,128)(2,1)} fusion(bf16[8192,4096]{1,0:T(8,128)(2,1)} %bitcast, bf16[4096,128]{1,0:T(8,128)(2,1)} %get-tuple-element.31, bf16[4096,128]{1,0:T(8,128)(2,1)} %get-tuple-element.30, bf16[4096,256]{1,0:T(8,128)(2,1)S(1)} %dynamic-slice_bitcast_fusion), kind=kOutput, calls=%fused_computation.6 | convolution fusion | flops 34376515584 | bytes 79691776 | tf_op jit(solution)/shard_map/dot_general | solution.py:47
  304.9 38.8 %attn_fwd.1 = (bf16[16,8,64,256]{3,2,1,0:T(8,128)(2,1)}, bf16[16,8,64,256]{3,2,1,0:T(8,128)(2,1)}, bf16[16,8,64,128]{3,2,1,0:T(8,128)(2,1)S(1)}, f32[8,2,1,1024]{3,2,1,0:T(1,128)S(1)}, f32[8,2,1,1024]{3,2,1,0:T(1,128)S(1)}) custom-call(bf16[16,8,64,512]{3,2,1,0:T(8,128)(2,1)} %bitcast.63, bf16[16,8,64,512]{3,2,1,0:T(8,128)(2,1)} %bitcast.64, ...), custom_call_target="tpu_custom_call" | custom-call | flops 4294967296 | bytes 20971520 | tf_op jit(solution)/shard_map/attn_fwd/pallas_call | solution.py:146
  345.0 161.8 %all-gather.18.cloned.1.call-done = bf16[128,64,4096]{2,1,0:T(8,128)(2,1)} async-done(((bf16[8,64,4096]{2,1,0:T(8,128)(2,1)}), bf16[128,64,4096]{2,1,0:T(8,128)(2,1)}) %all-gather.18.cloned.1.call-update) | async-done | bytes 67108880 | tf_op jit(solution)/shard_map/all_gather | solution.py:283
  506.8 28.5 %convolution_bitcast_fusion.1 = f32[256,4096]{1,0:T(8,128)} fusion(bf16[16,8,64,256]{3,2,1,0:T(8,128)(2,1)} %get-tuple-element.15, bf16[16,8,64,4096]{3,2,1,0:T(8,128)(2,1)} %bitcast.13), kind=kOutput, calls=%fused_computation.25 | convolution fusion | flops 17179869184 | bytes 75497472 | tf_op jit(solution)/shard_map/dot_general | solution.py:47
  535.3 31.5 %convert_bitcast_fusion.g_ref = bf16[16,8,64,256]{3,2,1,0:T(8,128)(2,1)} fusion(bf16[16,8,64,4096]{3,2,1,0:T(8,128)(2,1)} %bitcast.13, bf16[4096,4096]{1,0:T(8,128)(2,1)} %param.10, s32[]{:T(128)S(6)} %select_n.39), kind=kOutput, calls=%fused_computation.36 | convolution fusion | flops 17181966336 | bytes 73400320 | tf_op jit(solution)/shard_map/ibsd,cd->ibsc/dot_general | solution.py:304
  566.8 53.6 %attn_bwd.1 = (bf16[16,8,64,256]{3,2,1,0:T(8,128)(2,1)}, bf16[16,8,64,128]{3,2,1,0:T(8,128)(2,1)S(1)}, bf16[16,8,64,128]{3,2,1,0:T(8,128)(2,1)S(1)}) custom-call(bf16[16,8,64,256]{3,2,1,0:T(8,128)(2,1)} %get-tuple-element.16.q_ref, bf16[16,8,64,128]{3,2,1,0:T(8,128)(2,1)} %copy-done.2, bf16[16,8,64,512]{3,2,1,0:T(8,128)(2,1)} %bitcast.66, ...), custom_call_target="tpu_custom_call" | custom-call | flops 10737418240 | bytes 20971520 | tf_op jit(solution)/shard_map/attn_bwd/pallas_call | solution.py:163
  632.5 3.8 fusion.23
  636.3 40.4 %convolution_bitcast_fusion = f32[4096,384]{1,0:T(8,128)S(1)} fusion(bf16[16,8,64,4096]{3,2,1,0:T(8,128)(2,1)} %bitcast.21, bf16[16,8,64,128]{3,2,1,0:T(8,128)(2,1)S(1)} %fusion.23, bf16[16,8,64,256]{3,2,1,0:T(8,128)(2,1)S(1)} %copy-done.7), kind=kOutput, calls=%fused_computation.24 | convolution fusion | flops 25782386688 | bytes 79691776 | tf_op jit(solution)/shard_map/dot_general | solution.py:47
  682.0 3.3 all-to-all-start
  685.3 6.4 pad_maximum_fusion
  691.7 55.2 %all-to-all-done = bf16[16,8,64,256]{3,2,1,0:T(8,128)(2,1)} async-done(((bf16[16,8,64,256]{3,2,1,0:T(8,128)(2,1)}), bf16[16,8,64,256]{3,2,1,0:T(8,128)(2,1)}, u32[]{:S(2)}, u32[]{:S(2)}) %all-to-all-start) | async-done | bytes 4194336 | tf_op jit(solution)/shard_map/all_to_all | solution.py:299
  746.9 4.4 all-to-all-start.1
  751.4 26.5 %bitcast_convert_fusion.1 = bf16[8,64,4096]{2,1,0:T(8,128)(2,1)} fusion(bf16[16,8,64,256]{3,2,1,0:T(8,128)(2,1)} %all-to-all-done, bf16[16,256,4096,1]{2,1,3,0:T(8,128)(2,1)} %bitcast.72), kind=kOutput, calls=%fused_computation.21 | convolution fusion | flops 17181966336 | bytes 41943040 | tf_op jit(solution)/shard_map/ibsc,icd->bsd/dot_general | solution.py:324
  777.9 65.6 %all-to-all-done.1 = bf16[16,8,64,384]{3,2,1,0:T(8,128)(2,1)} async-done(((bf16[16,8,64,384]{3,2,1,0:T(8,128)(2,1)}), bf16[16,8,64,384]{3,2,1,0:T(8,128)(2,1)}, u32[]{:S(2)}, u32[]{:S(2)}) %all-to-all-start.1) | async-done | bytes 6291488 | tf_op jit(solution)/shard_map/all_to_all | solution.py:314
  843.5 40.2 %convert_reduce_fusion = (f32[4096]{0:T(1024)S(1)}, f32[8,64]{1,0:T(8,128)S(1)}, bf16[8,64,4096]{2,1,0:T(8,128)(2,1)}) fusion(f32[4096]{0:T(1024)S(1)} %copy-done.9, f32[8,64]{1,0:T(8,128)S(1)} %copy-done.11, bf16[8,64,4096]{2,1,0:T(8,128)(2,1)} %param.7, bf16[16,8,64,384]{3,2,1,0:T(8,128)(2,1)} %all-to-all-done.1, bf16[16,4096,384]{2,1,0:T(8,128)(2,1)} %split.1), kind=kOutput, calls=%fused_computation.3 | convolution fusion | flops 25786576896 | bytes 65048576 | tf_op jit(solution)/shard_map/ibsc,idc->bsd/dot_general | solution.py:325
  883.8 6.2 fusion.12
  889.9 34.7 %all-reduce.1 = (f32[4096]{0:T(1024)}, f32[4096]{0:T(1024)}) all-reduce(f32[4096]{0:T(1024)S(1)} %get-tuple-element.24, f32[4096]{0:T(1024)S(1)} %get-tuple-element.26), channel_id=1, replica_groups=mesh['sp'=16] {'sp'}, use_global_device_ids=true, to_apply=%region_5.6 | all-reduce | flops 8192 | bytes 65536 | tf_op jit(solution)/shard_map/psum | solution.py:327
  924.7 7.2 add_convert_fusion
  931.8 27.5 %place.4.old_ref = f32[196608,128]{1,0:T(8,128)} custom-call(f32[16,1024,384]{2,1,0:T(8,128)} %bitcast.70), custom_call_target="tpu_custom_call" | custom-call | flops 12582912000 | bytes 50331648 | tf_op jit(solution)/shard_map/place/pallas_call | solution.py:235
  959.3 39.6 %all-gather.24.cloned.1.call-done = f32[16384,384]{1,0:T(8,128)} async-done(((f32[1024,384]{1,0:T(8,128)}), f32[16384,384]{1,0:T(8,128)}) %all-gather.24.cloned.1.call-update) | async-done | bytes 25165840 | tf_op jit(solution)/shard_map/all_gather | solution.py:320
  998.9 27.8 %place.5.old_ref = f32[196608,128]{1,0:T(8,128)} custom-call(f32[16,1024,384]{2,1,0:T(8,128)} %bitcast.67, f32[196608,128]{1,0:T(8,128)} %place.4.old_ref), custom_call_target="tpu_custom_call", output_to_operand_aliasing={{}: (1, {})} | custom-call | flops 12582912000 | bytes 50331648 | tf_op jit(solution)/shard_map/place/pallas_call | solution.py:235
  1026.7 78.1 %all-gather.22.cloned.1.call-done = f32[16384,384]{1,0:T(8,128)} async-done(((f32[1024,384]{1,0:T(8,128)}), f32[16384,384]{1,0:T(8,128)}) %all-gather.22.cloned.1.call-update) | async-done | bytes 25165840 | tf_op jit(solution)/shard_map/all_gather | solution.py:320
  1104.8 27.8 %place.6.old_ref = f32[196608,128]{1,0:T(8,128)} custom-call(f32[16,1024,384]{2,1,0:T(8,128)} %bitcast.68, f32[196608,128]{1,0:T(8,128)} %place.5.old_ref), custom_call_target="tpu_custom_call", output_to_operand_aliasing={{}: (1, {})} | custom-call | flops 12582912000 | bytes 50331648 | tf_op jit(solution)/shard_map/place/pallas_call | solution.py:235
  1132.6 78.1 %all-gather.20.cloned.1.call-done = f32[16384,384]{1,0:T(8,128)} async-done(((f32[1024,384]{1,0:T(8,128)}), f32[16384,384]{1,0:T(8,128)}) %all-gather.20.cloned.1.call-update) | async-done | bytes 25165840 | tf_op jit(solution)/shard_map/all_gather | solution.py:320
  1210.7 27.6 %place.7 = f32[196608,128]{1,0:T(8,128)} custom-call(f32[16,1024,384]{2,1,0:T(8,128)} %bitcast.69, f32[196608,128]{1,0:T(8,128)} %place.6.old_ref), custom_call_target="tpu_custom_call", output_to_operand_aliasing={{}: (1, {})} | custom-call | flops 12582912000 | bytes 50331648 | tf_op jit(solution)/shard_map/place/pallas_call | solution.py:235
  1238.3 216.7 %all-gather.14.cloned.1.call-done.in_ref = f32[4096,4096]{1,0:T(8,128)} async-done(((f32[256,4096]{1,0:T(8,128)}), f32[4096,4096]{1,0:T(8,128)}) %all-gather.14.cloned.1.call-update) | async-done | bytes 67108880 | tf_op jit(solution)/shard_map/all_gather | solution.py:302
  1455.1 44.6 %shard_map.118 = f32[4096,4096]{1,0:T(8,128)} custom-call(f32[4096,4096]{1,0:T(8,128)} %all-gather.14.cloned.1.call-done.in_ref), custom_call_target="tpu_custom_call" | custom-call | flops 33554432000 | bytes 134217728 | tf_op jit(solution)/shard_map/pallas_call | solution.py:255
  (83 shorter events, 29.4 us)
Async XLA Ops:
  7.2 255.3 %all-gather.16.cloned.1.call-start = ((), (), s32[]{:S(2)}) async-start(), calls=%async_computation.3 | async-start | bytes 71303168 | tf_op jit(solution)/shard_map/all_gather | solution.py:282
  7.2 3.5 copy-start.3
  7.2 5.9 copy-start.8
  7.2 5.9 copy-start.18
  10.7 1.8 copy-start.10
  11.9 0.6 copy-start.16
  12.5 0.6 copy-start.12
  16.5 0.9 copy-start.21
  16.5 490.3 %all-gather.18.cloned.1.call-start = ((), (), s32[]{:S(2)}) async-start(), calls=%async_computation.4 | async-start | bytes 71303168 | tf_op jit(solution)/shard_map/all_gather | solution.py:283
  17.2 914.6 %all-gather.26.cloned.1.call-start = ((), (), s32[]{:S(2)}) async-start(), calls=%async_computation.8 | async-start | bytes 26738688 | tf_op jit(solution)/shard_map/all_gather | solution.py:320
  53.9 1.9 copy-start.14
  53.9 1.9 copy-start.19
  343.7 1.3 copy-start.2
  620.5 1.3 copy-start
  620.5 3.1 copy-start.15
  620.5 3.2 copy-start.20
  623.3 4.5 collective-permute-start
  630.8 1.7 copy-start.1
  632.5 3.8 copy-start.7
  636.3 40.4 %copy-start.5 = (bf16[16,8,64,128]{3,2,1,0:T(8,128)(2,1)}, bf16[16,8,64,128]{3,2,1,0:T(8,128)(2,1)S(1)}, u32[]{:S(2)}) copy-start(bf16[16,8,64,128]{3,2,1,0:T(8,128)(2,1)S(1)} %fusion.23) | copy-start | bytes 6291460
  679.5 319.4 %all-gather.24.cloned.1.call-start = ((), (), s32[]{:S(2)}) async-start(), calls=%async_computation.7 | async-start | bytes 26738688 | tf_op jit(solution)/shard_map/all_gather | solution.py:320
  680.0 424.8 %all-gather.22.cloned.1.call-start = ((), (), s32[]{:S(2)}) async-start(), calls=%async_computation.6 | async-start | bytes 26738688 | tf_op jit(solution)/shard_map/all_gather | solution.py:320
  680.6 530.1 %all-gather.20.cloned.1.call-start = ((), (), s32[]{:S(2)}) async-start(), calls=%async_computation.5 | async-start | bytes 26738688 | tf_op jit(solution)/shard_map/all_gather | solution.py:320
  681.2 4.1 copy-start.6
  681.2 773.9 %all-gather.14.cloned.1.call-start = ((), (), s32[]{:S(2)}) async-start(), calls=%async_computation.2 | async-start | bytes 71303168 | tf_op jit(solution)/shard_map/all_gather | solution.py:302
  682.0 64.9 %all-to-all-start = ((bf16[16,8,64,256]{3,2,1,0:T(8,128)(2,1)}), bf16[16,8,64,256]{3,2,1,0:T(8,128)(2,1)}, u32[]{:S(2)}, u32[]{:S(2)}) async-start(bf16[16,8,64,256]{3,2,1,0:T(8,128)(2,1)} %get-tuple-element.15), calls=%async_computation | async-start | bytes 8388608 | tf_op jit(solution)/shard_map/all_to_all | solution.py:299
  746.9 96.7 %all-to-all-start.1 = ((bf16[16,8,64,384]{3,2,1,0:T(8,128)(2,1)}), bf16[16,8,64,384]{3,2,1,0:T(8,128)(2,1)}, u32[]{:S(2)}, u32[]{:S(2)}) async-start(bf16[16,8,64,384]{3,2,1,0:T(8,128)(2,1)} %pad_maximum_fusion), calls=%async_computation.1 | async-start | bytes 12582912 | tf_op jit(solution)/shard_map/all_to_all | solution.py:314
  751.3 92.2 %copy-start.9 = (f32[4096]{0:T(1024)S(1)}, f32[4096]{0:T(1024)}, u32[]{:S(2)}) copy-start(f32[4096]{0:T(1024)} %param.11) | copy-start | bytes 49156
  751.4 92.2 %copy-start.11 = (f32[8,64]{1,0:T(8,128)S(1)}, f32[8,64]{1,0:T(8,128)}, u32[]{:S(2)}) copy-start(f32[8,64]{1,0:T(8,128)} %copy-done.10) | copy-start | bytes 6148
  777.9 105.8 %copy-start.17 = (f32[8,64]{1,0:T(8,128)S(1)}, f32[8,64]{1,0:T(8,128)}, u32[]{:S(2)}) copy-start(f32[8,64]{1,0:T(8,128)} %copy-done.16) | copy-start | bytes 6148
  777.9 105.8 %copy-start.13 = (f32[8,64]{1,0:T(8,128)S(1)}, f32[8,64]{1,0:T(8,128)}, u32[]{:S(2)}) copy-start(f32[8,64]{1,0:T(8,128)} %copy-done.12) | copy-start | bytes 6148
  843.5 40.2 %copy-start.4 = (bf16[8,64,4096]{2,1,0:T(8,128)(2,1)S(1)}, bf16[8,64,4096]{2,1,0:T(8,128)(2,1)}, u32[]{:S(2)}) copy-start(bf16[8,64,4096]{2,1,0:T(8,128)(2,1)} %param.7) | copy-start | bytes 12582916
Sparse Core Ops, SparseCore 0:
  16.6 245.8 all-gather.15
  264.7 242.0 all-gather.17
  679.6 212.7 all-gather.25
  894.5 104.3 all-gather.23
  1001.0 103.7 all-gather.21
  1106.9 103.7 all-gather.19
  1213.0 242.0 all-gather.13
